TPU v7x, 512 devices: a whole 4x4x16 slice. The times are simulated.
512 devices in a mesh: grp: 16 (over y, z_hi, core), dev: 32 (over z_lo, x).
Axes of the slice: x: 4, y: 4, z: 16 (z_hi: 2, z_lo: 8; z = z_hi * 8 + z_lo), core: 2. Of those that a mesh axis runs over, the one named last changes fastest.
Arguments:
- train_grads: bfloat16 [65536, 1024], P(('grp', 'dev')), may hold values from -192 to 192, as said below
- queries: bfloat16 [2048, 1024], P('grp'), may hold values from -6 to 6
Outputs:
- scores: bfloat16 [65536, 2048], P(('grp', 'dev'))
Inputs may be any that keep to these rules, and one draw needn't show every extreme that they name: `train_grads`: Real-valued projected gradients whose columns and rows differ in scale.
All inputs are finite; a program needn't handle non-finite values. Where the computation divides by a largest or mean magnitude, that divisor is 1e-20 or more.
Results may differ from a plain program's by a relative error of at most 0.001.
The roundings to bfloat16 on the way count: a program that leaves them out, or rounds other values in their place, can miss the bound.
Values may be sent and summed in bfloat16 or wider, within the bound.
A program may use at most 64 MiB of HBM per device.

v0:
```python
import jax
import jax.numpy as jnp
from jax import lax
from jax.sharding import PartitionSpec as P

ITERS = 8


damping_ratio = 0.1


def copy_for_each(array, axis):
    copies = jnp.broadcast_to(array, (lax.axis_size(axis), *array.shape))
    return lax.all_to_all(copies, axis, split_axis=0, concat_axis=0, tiled=True)


def laid_out(pieces, dim):
    dims = list(pieces.shape[1:])
    dims[dim] *= pieces.shape[0]
    return jnp.moveaxis(pieces, 0, dim).reshape(dims)


def gather_directly(array, axis, dim):
    pieces = copy_for_each(array, axis)
    return laid_out(pieces, dim)


def local_solve(gram, own, total, width):
    normed = gram / total
    damp = damping_ratio * jnp.trace(gram) / (total * width)
    bound = jnp.max(jnp.sum(jnp.abs(normed), axis=1)) + damp
    step = 1.0 / bound
    oper = normed + damp * jnp.eye(width, dtype=jnp.float32)
    state = step * own
    for index in range(ITERS):
        state = state + step * (own - jnp.dot(state, oper, precision=lax.Precision.HIGHEST))
    return state.astype(jnp.bfloat16)


def body(train_grads, queries):
    rows, width = train_grads.shape
    ndevice = lax.axis_size("dev")
    total = rows * ndevice * lax.axis_size("grp")
    qvals = queries.astype(jnp.float32)
    qrows = qvals.shape[0] // ndevice
    qstart = lax.axis_index("dev") * qrows
    own = lax.dynamic_slice_in_dim(qvals, qstart, qrows, 0)
    gram = lax.psum(
        lax.dot_general(
            train_grads, train_grads, (((0,), (0,)), ((), ())), preferred_element_type=jnp.float32
        ),
        ("grp", "dev"),
    )
    mine = local_solve(gram, own, total, width)
    prepared = gather_directly(mine, "dev", 0)
    return lax.dot_general(
        train_grads,
        lax.all_gather(prepared, "grp", axis=0, tiled=True),
        (((1,), (1,)), ((), ())),
        preferred_element_type=jnp.float32,
    ).astype(jnp.bfloat16)


def solution(mesh):
    return jax.shard_map(
        body,
        mesh=mesh,
        in_specs=(P(("grp", "dev"), None), P("grp", None)),
        out_specs=P(("grp", "dev"), None),
        check_vma=False,
    )
```

profile of v0, /device:TPU:1, one launch (start us, length us, event | category | flops | bytes accessed | tf_op | source)
XLA Modules:
  0.0 696.8 jit_solution(398364279938283323)
XLA Ops:
  6.5 0.0 copy-start
  6.5 0.0 all-reduce.2.cloned.1.call-start
  6.5 0.9 copy-done
  7.5 2.7 fusion.19
  10.2 0.0 all-reduce.2.cloned.1.call-update
  10.2 0.0 all-gather.2.cloned.1.call-start
  10.3 500.9 %all-reduce.2.cloned.1.call-done = f32[1024,1024]{1,0:T(8,128)} async-done(((f32[1024,1024]{1,0:T(8,128)}), f32[1024,1024]{1,0:T(8,128)}) %all-reduce.2.cloned.1.call-update) | async-done | bytes 4194320 | tf_op jit(solution)/shard_map/psum | solution.py:48
  511.2 3.3 select_reduce_fusion
  515.2 0.6 reduce_max.9
  516.5 0.0 copy-start.1
  516.5 4.6 fusion.16
  521.1 0.0 copy-done.1
  521.1 3.0 fusion.14
  524.1 3.0 fusion.12
  527.0 3.0 fusion.10
  530.0 3.0 fusion.8
  532.9 3.1 fusion.6
  536.1 3.0 fusion.4
  539.0 3.0 fusion.17
  542.0 0.1 broadcast_in_dim.8
  542.1 31.9 %all_to_all.5 = bf16[32,4,1024]{2,1,0:T(4,128)(2,1)S(1)} all-to-all(bf16[32,4,1024]{2,1,0:T(4,128)(2,1)S(1)} %broadcast_in_dim.8), channel_id=1, replica_groups=mesh['grp'=16,'dev'=32] {'dev'}, dimensions={0} | all-to-all | bytes 524288 | tf_op jit(solution)/shard_map/all_to_all | solution.py:14
  574.0 0.8 reshape.3
  574.8 0.0 all-gather.2.cloned.1.call-update
  574.8 110.7 %all-gather.2.cloned.1.call-done = bf16[2048,1024]{1,0:T(8,128)(2,1)} async-done(((bf16[128,1024]{1,0:T(8,128)(2,1)}), bf16[2048,1024]{1,0:T(8,128)(2,1)}) %all-gather.2.cloned.1.call-update) | async-done | bytes 4194320 | tf_op jit(solution)/shard_map/all_gather | solution.py:58
  685.5 3.4 fusion
  689.0 1.0 copy.3
Async XLA Ops:
  6.5 1.0 copy-start
  6.5 504.7 %all-reduce.2.cloned.1.call-start = ((), (), s32[]{:S(2)}) async-start(), calls=%async_computation.1 | async-start | bytes 8388608 | tf_op jit(solution)/shard_map/psum | solution.py:48
  10.2 675.3 %all-gather.2.cloned.1.call-start = ((), (), s32[]{:S(2)}) async-start(), calls=%async_computation.2 | async-start | bytes 4456448 | tf_op jit(solution)/shard_map/all_gather | solution.py:58
  516.5 4.6 copy-start.1
Sparse Core Ops, SparseCore 0:
  12.8 498.3 all-reduce.1
  574.9 110.5 all-gather.1
where the time goes:
time: 698 us; the launch traced here: 697 us
  waiting for transfers between devices  612 us (88%)
  blocking collectives  31.9 us (5%)
  matrix products  31.6 us (5%)
  between operations  14.8 us (2%)
    psum x1, waiting for transfers between devices, body(): lax.psum(lax.dot_general(train_grads, train_grads, (((0,), (0,)), ((), ()...  501 us
    all_gather x1, waiting for transfers between devices, body(): lax.all_gather(prepared, 'grp', axis=0, tiled=True)  111 us
    all_to_all x1, blocking collectives, copy_for_each(): return lax.all_to_all(copies, axis, split_axis=0, concat_axis=0, tiled=True)  31.9 us
    dot_general x8, matrix products, local_solve(): jnp.dot(state, oper, precision=lax.Precision.HIGHEST)  25.5 us
  transfers between devices with their start and end apart: 2, of which 2 were waited for; matrix products, arithmetic and copies ran while one was open for 0% of the time, Pallas kernels for 0%

commit v1 on v0

v1 whole, which is shorter than its diff:
```python
import jax
import jax.numpy as jnp
from jax import lax
from jax.experimental import pallas as pl
from jax.experimental.pallas import tpu as pltpu
from jax.sharding import PartitionSpec as P

MESH = pl.DeviceIdType.MESH
F32, BF16 = jnp.float32, jnp.bfloat16
ITERS = 8
DAMPING = 0.1
K = 1024
ROWS = 128
NB = K // 128
NX = NY = 4
NZ = 16
OWNED = ((0, 3, 4, 7), (1, 2, 5, 6))
SLOTS = {}
for _core, _rows in enumerate(OWNED):
    for _slot, _ij in enumerate((i, j) for i in _rows for j in range(i, NB)):
        SLOTS[_ij] = (_core, _slot)
NSLOT = 18
HELD = NSLOT * 128
HALF = HELD // 2
BIG = HALF // 4
SMALL = BIG // 4
TILES = 2 * SMALL // 8
CUT_BIG = (0, 144, 288)
CUT_SMALL = (0, 40, 72)
NSEM = 256


def split3(value):
    first = value.astype(BF16)
    rest = value - first.astype(F32)
    second = rest.astype(BF16)
    third = (rest - second.astype(F32)).astype(BF16)
    return first, second, third


def nt_dot(left, right):
    return lax.dot_general(left, right, (((1,), (1,)), ((), ())), preferred_element_type=F32)


def kernel(
    t_hbm, q_hbm, out_ref,
    tt, qb, part, held, r1, r2, s1, s2, zr, zr2, g0, g1, g2, colsum, xs, ys, pa,
    send_sem, recv_sem, local_sem,
):
    grp, dev = lax.axis_index("grp"), lax.axis_index("dev")
    y, zh, core = grp // 4, (grp // 2) % 2, grp % 2
    x, z = dev % 4, zh * 8 + dev // 4

    def where(px, py, pz, pc):
        return (py * 4 + (pz // 8) * 2 + pc, (pz % 8) * 4 + px)

    other = where(x, y, z, 1 - core)
    xp, xm = where((x + 1) % 4, y, z, core), where((x + 3) % 4, y, z, core)
    yp, ym = where(x, (y + 1) % 4, z, core), where(x, (y + 3) % 4, z, core)
    zs = [where(x, y, (z + d) % NZ, core) for d in range(NZ)]
    far = where(x, y, (z + 8) % NZ, core)

    started = []
    used = [0]

    def sems(n=1):
        base = used[0]
        used[0] += n
        assert used[0] <= NSEM
        return base

    def copy(src, dst, device, send, recv):
        return pltpu.make_async_remote_copy(
            src_ref=src, dst_ref=dst, send_sem=send_sem.at[send], recv_sem=recv_sem.at[recv],
            device_id=device, device_id_type=MESH,
        )

    def push(src, dst, device, send, recv=None):
        made = copy(src, dst, device, send, send if recv is None else recv)
        made.start()
        started.append(made)
        return made

    barrier = pltpu.get_barrier_semaphore()
    peers = [other, xp, xm, yp, ym] + zs[1:]
    for peer in peers:
        pl.semaphore_signal(barrier, inc=1, device_id=peer, device_id_type=MESH)
    mine_t = tt.at[pl.ds(pl.multiple_of(core * ROWS, ROWS), ROWS)]
    load_t = pltpu.make_async_copy(t_hbm, mine_t, local_sem.at[0])
    load_q = pltpu.make_async_copy(
        q_hbm.at[pl.ds(pl.multiple_of(x * 32, 32), 32)], qb.at[zh], local_sem.at[1]
    )
    load_t.start()
    load_q.start()
    load_t.wait()
    load_q.wait()
    pl.semaphore_wait(barrier, len(peers))

    send_t = push(mine_t, mine_t, other, sems())
    send_q = push(qb.at[zh], qb.at[zh], far, sems())
    send_t.wait_recv()

    def gram_rows(rows, cols):
        left = tt[:, rows * 128 : (rows + 1) * 128]
        right = tt[:, cols[0] * 128 : (cols[-1] + 1) * 128]
        return lax.dot_general(left, right, (((0,), (0,)), ((), ())), preferred_element_type=F32)

    for which in (0, 1):

        @pl.when(core == which)
        def _():
            for i in OWNED[which]:
                cols = list(range(i, NB))
                block = gram_rows(i, cols)
                for at, j in enumerate(cols):
                    slot = SLOTS[i, j][1]
                    part[slot * 128 : (slot + 1) * 128, :] = block[:, at * 128 : (at + 1) * 128]

    class Reduce:
        def __init__(self, base, cut, at, plus, minus, recv1, recv2, color):
            self.base, self.cut, self.at, self.plus, self.minus = base, cut, at, plus, minus
            self.r1, self.r2 = recv1, recv2
            self.color, self.sem = color, sems(6)
            self.moves = {}

        def piece(self, which, half):
            lo, hi = self.cut[half], self.cut[half + 1]
            row = self.base + which * self.cut[2] + lo
            return part.at[pl.ds(pl.multiple_of(row, 8), hi - lo)]

        def first(self, side):
            half = side
            return self.r1.at[self.color, side, pl.ds(0, self.cut[half + 1] - self.cut[half])]

        def second(self, side, half):
            lo, hi = self.cut[half], self.cut[half + 1]
            return self.r2.at[self.color, side, pl.ds(lo, hi - lo)]

        def start(self):
            a, s = self.at, self.sem
            self.moves[0] = push(self.piece((a + 2) % 4, 0), self.first(0), self.plus, s)
            self.moves[1] = push(self.piece((a + 2) % 4, 1), self.first(1), self.minus, s + 1)
            self.moves[2] = push(self.piece((a + 1) % 4, 1), self.second(0, 1), self.plus, s + 2)
            self.moves[3] = push(self.piece((a + 3) % 4, 0), self.second(1, 0), self.minus, s + 3)

        def middle(self):
            a, s = self.at, self.sem
            self.moves[0].wait_recv()
            mine = self.piece((a + 1) % 4, 0)
            mine[...] = mine[...] + self.first(0)[...]
            self.moves[1].wait_recv()
            mine1 = self.piece((a + 3) % 4, 1)
            mine1[...] = mine1[...] + self.first(1)[...]
            self.moves[4] = push(mine, self.second(0, 0), self.plus, s + 4)
            self.moves[5] = push(mine1, self.second(1, 1), self.minus, s + 5)

        def finish(self):
            for n in (2, 3, 4, 5):
                self.moves[n].wait_recv()
            row = self.base + self.at * self.cut[2]
            mine = part.at[pl.ds(pl.multiple_of(row, 8), self.cut[2])]
            total = mine[...] + self.r2[self.color, 0] + self.r2[self.color, 1]
            return mine, total

    base_a, base_b = 0, HALF
    red = [
        Reduce(base_a, CUT_BIG, x, xp, xm, r1, r2, 0),
        Reduce(base_b, CUT_BIG, y, yp, ym, r1, r2, 1),
    ]
    for r in red:
        r.start()
    for r in red:
        r.middle()
    for r in red:
        mine, total = r.finish()
        mine[...] = total
    red = [
        Reduce(base_a + x * BIG, CUT_SMALL, y, yp, ym, s1, s2, 0),
        Reduce(base_b + y * BIG, CUT_SMALL, x, xp, xm, s1, s2, 1),
    ]
    for r in red:
        r.start()
    for r in red:
        r.middle()
    off_a = base_a + x * BIG + y * SMALL
    off_b = base_b + y * BIG + x * SMALL
    for r in red:
        mine, total = r.finish()
        mine[...] = total

    def row_of(tile):
        late = tile // 9
        row = (1 - late) * (off_a + tile * 8) + late * (off_b + (tile - 9) * 8)
        return pl.multiple_of(row, 8)

    def tile_of(ref, tile):
        return ref.at[pl.ds(row_of(tile), 8)]

    my_held = held.at[core]
    sz_send, sz_recv = sems(NZ), sems(NZ)
    sz2_send, sz2_recv = sems(NZ), sems(NZ)
    late_sends = []
    for d in range(1, NZ):
        dest = (z + d) % NZ
        push(tile_of(part, dest), zr.at[z], zs[d], sz_send + d, sz_recv + z)
    for d in range(1, NZ):
        dest = (z + d) % NZ

        @pl.when(dest < TILES - NZ)
        def _():
            copy(tile_of(part, dest + NZ), zr2.at[z], zs[d], sz2_send + d, sz2_recv + z).start()

    zr[z] = part[pl.ds(row_of(z), 8), :]
    for d in range(1, NZ):
        src = (z + NZ - d) % NZ
        copy(zr.at[src], zr.at[src], zs[d], sz_send + d, sz_recv + src).wait_recv()
    total = zr[0]
    for n in range(1, NZ):
        total = total + zr[n]
    my_held[pl.ds(row_of(z), 8), :] = total

    @pl.when(z < TILES - NZ)
    def _():
        zr2[z] = part[pl.ds(row_of(z + NZ), 8), :]
        for d in range(1, NZ):
            src = (z + NZ - d) % NZ
            copy(zr2.at[src], zr2.at[src], zs[d], sz2_send + d, sz2_recv + src).wait_recv()
        total = zr2[0]
        for n in range(1, NZ):
            total = total + zr2[n]
        my_held[pl.ds(row_of(z + NZ), 8), :] = total

    gz_send, gz_recv = sems(NZ), sems(NZ)
    gz2_send, gz2_recv = sems(NZ), sems(TILES - NZ)
    mine = tile_of(my_held, z)
    for d in range(1, NZ):
        push(mine, mine, zs[d], gz_send + d, gz_recv + z)

    @pl.when(z < TILES - NZ)
    def _():
        mine = tile_of(my_held, z + NZ)
        for d in range(1, NZ):
            copy(mine, mine, zs[d], gz2_send + d, gz2_recv + z).start()

    for d in range(1, NZ):
        src = (z + NZ - d) % NZ
        got = tile_of(my_held, src)
        copy(got, got, zs[d], gz_send + d, gz_recv + src).wait_recv()
    for n in range(TILES - NZ):

        @pl.when(z != n)
        def _():
            got = tile_of(my_held, n + NZ)
            copy(got, got, zs[1], gz2_send + 1, gz2_recv + n).wait_recv()

    class Gather:
        def __init__(self, get, at, plus, minus):
            self.get, self.at, self.plus, self.minus, self.sem = get, at, plus, minus, sems(6)

        def start(self):
            g, a, s = self.get, self.at, self.sem
            push(g(a, 0), g(a, 0), self.plus, s)
            push(g(a, 1), g(a, 1), self.minus, s + 2)
            push(g(a, 1), g(a, 1), self.plus, s + 1)
            push(g(a, 0), g(a, 0), self.minus, s + 3)

        def got(self, which, half, n):
            ref = self.get(which % 4, half)
            copy(ref, ref, self.plus, self.sem + n, self.sem + n).wait_recv()
            return ref

        def middle(self):
            a, s = self.at, self.sem
            ref = self.got(a + 3, 0, 0)
            push(ref, ref, self.plus, s + 4)
            ref = self.got(a + 1, 1, 2)
            push(ref, ref, self.minus, s + 5)

        def near(self):
            self.got(self.at + 3, 1, 1)
            self.got(self.at + 1, 0, 3)

        def finish(self):
            self.got(self.at + 2, 0, 4)
            self.got(self.at + 2, 1, 5)

    def rows(base, cut):
        def get(which, half):
            lo, hi = cut[half], cut[half + 1]
            return my_held.at[pl.ds(pl.multiple_of(base + which * cut[2] + lo, 8), hi - lo)]

        return get

    def both(gathers):
        for g in gathers:
            g.start()
        for g in gathers:
            g.middle()

    pair = []

    def hand_over(ref):
        pair.append(push(ref, ref, other, sems()))

    stage = [
        Gather(rows(base_a + x * BIG, CUT_SMALL), y, yp, ym),
        Gather(rows(base_b + y * BIG, CUT_SMALL), x, xp, xm),
    ]
    both(stage)
    for g in stage:
        g.near()
        g.finish()

    def big(base, which):
        return my_held.at[pl.ds(pl.multiple_of(base + (which % 4) * BIG, 8), BIG)]

    bases = ((base_a, x), (base_b, y))
    stage = [
        Gather(rows(base_a, CUT_BIG), x, xp, xm),
        Gather(rows(base_b, CUT_BIG), y, yp, ym),
    ]
    both(stage)
    for base, a in bases:
        hand_over(big(base, a))
    for g, (base, a) in zip(stage, bases):
        g.near()
        hand_over(big(base, a + 3))
        hand_over(big(base, a + 1))
    for g, (base, a) in zip(stage, bases):
        g.finish()
        hand_over(big(base, a + 2))
    for made in pair:
        made.wait_recv()

    colsum[...] = jnp.zeros_like(colsum)
    trace = jnp.zeros((8, 128), F32)
    row_id = lax.broadcasted_iota(jnp.int32, (128, 128), 0)
    col_id = lax.broadcasted_iota(jnp.int32, (128, 128), 1)

    def place(block, i, j):
        at = (slice(i * 128, (i + 1) * 128), slice(j * 128, (j + 1) * 128))
        for plane, value in zip((g0, g1, g2), split3(block)):
            plane[at] = value
        colsum[:, at[1]] += jnp.sum(jnp.abs(block).reshape(16, 8, 128), axis=0)

    for i in range(NB):
        for j in range(i, NB):
            owner, slot = SLOTS[i, j]
            block = held[owner, slot * 128 : (slot + 1) * 128, :]
            place(block, i, j)
            if i == j:
                diag = jnp.where(row_id == col_id, block, 0.0)
                trace = trace + jnp.sum(diag.reshape(16, 8, 128), axis=0)
            else:
                place(block.T, j, i)

    total_rows = ROWS * lax.axis_size("grp") * lax.axis_size("dev")
    scale = 1.0 / total_rows
    trace = jnp.sum(jnp.sum(trace, axis=0, keepdims=True), axis=1, keepdims=True)
    damp = DAMPING * trace / (total_rows * K)
    sums = jnp.sum(colsum[...], axis=0, keepdims=True) * scale
    bound = jnp.max(sums, axis=1, keepdims=True) + damp
    step = 1.0 / bound

    send_q.wait_recv()

    def queries():
        return jnp.concatenate([qb[0], qb[1]], axis=0).astype(F32)

    ys[...] = step * queries()

    def iterate(_, carry):
        for n, value in enumerate(split3(ys[...])):
            xs[n * 64 : (n + 1) * 64, :] = value
        for n in range(4):
            at = slice(n * 256, (n + 1) * 256)
            low = jnp.dot(xs[0:64], g2[:, at], preferred_element_type=F32)
            mid = jnp.dot(xs[0:128], g1[:, at], preferred_element_type=F32)
            top = jnp.dot(xs[...], g0[:, at], preferred_element_type=F32)
            prod = top[0:64] + (top[64:128] + mid[0:64] + (top[128:192] + mid[64:128] + low))
            state = ys[:, at]
            query = jnp.concatenate([qb[0, :, at], qb[1, :, at]], axis=0).astype(F32)
            ys[:, at] = state + step * (query - (prod * scale + damp * state))
        return carry

    lax.fori_loop(0, ITERS, iterate, 0)
    pa[y, 0, core, x] = ys[0:32, :].astype(BF16)
    pa[y, 1, core, x] = ys[32:64, :].astype(BF16)

    pair = []
    hand_over(pa.at[y, 0, core, x])
    hand_over(pa.at[y, 1, core, x])
    stage = [
        Gather(lambda p, h: pa.at[y, 0, core, p, pl.ds(16 * h, 16)], x, xp, xm),
        Gather(lambda p, h: pa.at[p, 1, core, x, pl.ds(16 * h, 16)], y, yp, ym),
    ]
    both(stage)
    for g in stage:
        g.near()
        g.finish()
    stage = [
        Gather(lambda p, h: pa.at[p, 0, core, pl.ds(2 * h, 2)], y, yp, ym),
        Gather(lambda p, h: pa.at[pl.ds(2 * h, 2), 1, core, p], x, xp, xm),
    ]
    both(stage)
    for n in range(1, 4):
        hand_over(pa.at[y, 0, core, (x + n) % 4])
        hand_over(pa.at[(y + n) % 4, 1, core, x])
    for g in stage:
        g.near()
    for n in (3, 1):
        hand_over(pa.at[(y + n) % 4, 0, core])
        hand_over(pa.at[:, 1, core, (x + n) % 4])
    for g in stage:
        g.finish()
    hand_over(pa.at[(y + 2) % 4, 0, core])
    hand_over(pa.at[:, 1, core, (x + 2) % 4])
    for made in pair:
        made.wait_recv()

    own = tt[pl.ds(pl.multiple_of(core * ROWS, ROWS), ROWS), :]
    for yy in range(4):
        for half in range(2):
            block = pa[yy, half].reshape(256, K)
            at = (yy * 2 + half) * 256
            out_ref[:, at : at + 256] = nt_dot(own, block).astype(BF16)

    for made in started:
        made.wait_send()
    for d in range(1, NZ):
        dest = (z + d) % NZ

        @pl.when(dest < TILES - NZ)
        def _():
            copy(tile_of(part, dest + NZ), zr2.at[z], zs[d], sz2_send + d, sz2_recv + z).wait_send()

        @pl.when(z < TILES - NZ)
        def _():
            mine = tile_of(my_held, z + NZ)
            copy(mine, mine, zs[d], gz2_send + d, gz2_recv + z).wait_send()


def body(train_grads, queries):
    nquery = queries.shape[0] * lax.axis_size("grp")
    return pl.pallas_call(
        kernel,
        out_shape=jax.ShapeDtypeStruct((ROWS, nquery), BF16),
        in_specs=[pl.BlockSpec(memory_space=pl.ANY)] * 2,
        out_specs=pl.BlockSpec(memory_space=pltpu.VMEM),
        scratch_shapes=[
            pltpu.VMEM((2 * ROWS, K), BF16),
            pltpu.VMEM((2, 32, K), BF16),
            pltpu.VMEM((HELD, 128), F32),
            pltpu.VMEM((2, HELD, 128), F32),
            pltpu.VMEM((2, 2, BIG // 2, 128), F32),
            pltpu.VMEM((2, 2, BIG, 128), F32),
            pltpu.VMEM((2, 2, CUT_SMALL[1], 128), F32),
            pltpu.VMEM((2, 2, SMALL, 128), F32),
            pltpu.VMEM((NZ, 8, 128), F32),
            pltpu.VMEM((NZ, 8, 128), F32),
            pltpu.VMEM((K, K), BF16),
            pltpu.VMEM((K, K), BF16),
            pltpu.VMEM((K, K), BF16),
            pltpu.VMEM((8, K), F32),
            pltpu.VMEM((192, K), BF16),
            pltpu.VMEM((64, K), F32),
            pltpu.VMEM((4, 2, 2, 4, 32, K), BF16),
            pltpu.SemaphoreType.DMA((NSEM,)),
            pltpu.SemaphoreType.DMA((NSEM,)),
            pltpu.SemaphoreType.DMA((2,)),
        ],
        compiler_params=pltpu.CompilerParams(
            collective_id=0, has_side_effects=True, vmem_limit_bytes=48 * 1024 * 1024
        ),
    )(train_grads, queries)


def solution(mesh):
    return jax.shard_map(
        body,
        mesh=mesh,
        in_specs=(P(("grp", "dev"), None), P("grp", None)),
        out_specs=P(("grp", "dev"), None),
        check_vma=False,
    )
```

time: 698 us -> 106 us (0.15)
  waiting for transfers between devices: 612 us -> 0 us
  Pallas kernels: 0 us -> 103 us
  blocking collectives: 31.9 us -> 0 us
  matrix products: 31.6 us -> 0 us
  between operations: 14.8 us -> 0.01 us
    psum x1 -> x0, waiting for transfers between devices: 501 us -> none  [body(): lax.psum(lax.dot_general(train_grads, train_grads, (((0,), (0,)), ((), ()...]
    all_gather x1 -> x0, waiting for transfers between devices: 111 us -> none  [body(): lax.all_gather(prepared, 'grp', axis=0, tiled=True)]
    pallas_call x0 -> x1, Pallas kernels: none -> 103 us  [body(): pl.pallas_call(kernel, out_shape=jax.ShapeDtypeStruct((ROWS, nquery), BF1...]
    all_to_all x1 -> x0, blocking collectives: 31.9 us -> none  [copy_for_each(): return lax.all_to_all(copies, axis, split_axis=0, concat_axis=0, tiled=True)]
    dot_general x10 -> x0, matrix products: 31.6 us -> none  [the longest x8 25.5 us: local_solve(): jnp.dot(state, oper, precision=lax.Precision.HIGHEST)]
  transfers between devices with their start and end apart: 2 -> 0, of which waited for: 2 -> 0; matrix products, arithmetic and copies ran while one was open for 0% -> 0% of each run, Pallas kernels for 0% -> 0%
where the time goes in v1:
time: 106 us
  Pallas kernels  103 us (97%)
  local copies, waits for them, and re-layouts  2.69 us (3%)
    pallas_call x1, Pallas kernels, body(): pl.pallas_call(kernel, out_shape=jax.ShapeDtypeStruct((ROWS, nquery), BF1...  103 us
    unnamed x5, local copies, waits for them, and re-layouts  2.69 us

profile of v1, /device:TPU:1, one launch (start us, length us, event | category | flops | bytes accessed | tf_op | source)
XLA Modules:
  0.0 105.8 jit_solution(7662627817691955907)
XLA Ops:
  0.0 0.0 copy-start
  0.0 0.9 copy-done
  1.0 0.0 copy-start.1
  1.0 0.9 copy-done.1
  1.9 103.1 %shard_map.28 = bf16[128,2048]{1,0:T(8,128)(2,1)S(1)} custom-call(bf16[128,1024]{1,0:T(8,128)(2,1)S(1)} %copy-done, bf16[128,1024]{1,0:T(8,128)(2,1)S(1)} %copy-done.1), custom_call_target="tpu_custom_call" | custom-call | tf_op jit(solution)/shard_map/pallas_call | solution.py:445
  105.0 0.8 copy.4
Async XLA Ops:
  0.0 0.9 copy-start
  1.0 0.9 copy-start.1

commit v2 on v1

v2 whole, which is shorter than its diff:
```python
import jax
import jax.numpy as jnp
from jax import lax
from jax.experimental import pallas as pl
from jax.experimental.pallas import tpu as pltpu
from jax.sharding import PartitionSpec as P

MESH = pl.DeviceIdType.MESH
F32, BF16 = jnp.float32, jnp.bfloat16
ITERS = 8
DAMPING = 0.1
K = 1024
ROWS = 128
NB = K // 128
NX = NY = 4
NZ = 16
OWNED = ((0, 3, 4, 7), (1, 2, 5, 6))
SLOTS = {}
for _core, _rows in enumerate(OWNED):
    for _slot, _ij in enumerate((i, j) for i in _rows for j in range(i, NB)):
        SLOTS[_ij] = (_core, _slot)
NSLOT = 18
HELD = NSLOT * 128
HALF = HELD // 2
BIG = HALF // 4
SMALL = BIG // 4
TILES = 2 * SMALL // 8
CUT_BIG = (0, 144, 288)
CUT_SMALL = (0, 40, 72)
NSEM = 320
FAR_FIRST = sorted(range(1, NZ), key=lambda d: -min(d, NZ - d))


def split3(value):
    first = value.astype(BF16)
    rest = value - first.astype(F32)
    second = rest.astype(BF16)
    third = (rest - second.astype(F32)).astype(BF16)
    return first, second, third


def nt_dot(left, right):
    return lax.dot_general(left, right, (((1,), (1,)), ((), ())), preferred_element_type=F32)


def kernel(
    t_hbm, q_hbm, out_hbm,
    tt, tq, qv, qb, part, held, r1, r2, r3, zr, zr2, g0, g1, rest, colsum, xs, ys, pa, ob,
    send_sem, recv_sem, local_sem,
):
    grp, dev = lax.axis_index("grp"), lax.axis_index("dev")
    y, zh, core = grp // 4, (grp // 2) % 2, grp % 2
    x, z = dev % 4, zh * 8 + dev // 4

    def where(px, py, pz, pc):
        return (py * 4 + (pz // 8) * 2 + pc, (pz % 8) * 4 + px)

    other = where(x, y, z, 1 - core)
    xp, xm = where((x + 1) % 4, y, z, core), where((x + 3) % 4, y, z, core)
    yp, ym = where(x, (y + 1) % 4, z, core), where(x, (y + 3) % 4, z, core)
    xo, yo = where((x + 2) % 4, y, z, core), where(x, (y + 2) % 4, z, core)
    zs = [where(x, y, (z + d) % NZ, core) for d in range(NZ)]
    odd = z % 2
    neighbour = where(x, y, z + 1 - 2 * odd, core)
    near_half = (zh + odd) % 2
    far = where(x, y, (z + 8) % NZ, core)

    started = []
    used = [0]

    def sems(n=1):
        base = used[0]
        used[0] += n
        assert used[0] <= NSEM
        return base

    def copy(src, dst, device, send, recv):
        return pltpu.make_async_remote_copy(
            src_ref=src, dst_ref=dst, send_sem=send_sem.at[send], recv_sem=recv_sem.at[recv],
            device_id=device, device_id_type=MESH,
        )

    def push(src, dst, device, send, recv=None):
        made = copy(src, dst, device, send, send if recv is None else recv)
        made.start()
        started.append(made)
        return made

    barrier = pltpu.get_barrier_semaphore()
    peers = [other, xp, xm, xo, yp, ym, yo] + zs[1:]
    for peer in peers:
        pl.semaphore_signal(barrier, inc=1, device_id=peer, device_id_type=MESH)
    mine_t = tt.at[pl.ds(pl.multiple_of(core * ROWS, ROWS), ROWS)]
    load_t = pltpu.make_async_copy(t_hbm, mine_t, local_sem.at[0])
    load_q = pltpu.make_async_copy(q_hbm, qv, local_sem.at[1])
    load_own = pltpu.make_async_copy(t_hbm, tq.at[pl.ds(0, ROWS)], local_sem.at[2])
    load_t.start()
    load_q.start()
    load_own.start()
    load_t.wait()
    pl.semaphore_wait(barrier, len(peers))

    send_t = push(mine_t, mine_t, other, sems())
    send_near = push(mine_t, tq.at[pl.ds(ROWS, ROWS)], neighbour, sems())
    send_t.wait_recv()

    def gram_rows(rows, cols):
        left = tt[:, rows * 128 : (rows + 1) * 128]
        right = tt[:, cols[0] * 128 : (cols[-1] + 1) * 128]
        return lax.dot_general(left, right, (((0,), (0,)), ((), ())), preferred_element_type=F32)

    for which in (0, 1):

        @pl.when(core == which)
        def _():
            for i in OWNED[which]:
                cols = list(range(i, NB))
                block = gram_rows(i, cols)
                for at, j in enumerate(cols):
                    slot = SLOTS[i, j][1]
                    part[slot * 128 : (slot + 1) * 128, :] = block[:, at * 128 : (at + 1) * 128]

    class Reduce:
        def __init__(self, base, cut, at, plus, minus, recv1, recv2, color):
            self.base, self.cut, self.at, self.plus, self.minus = base, cut, at, plus, minus
            self.r1, self.r2 = recv1, recv2
            self.color, self.sem = color, sems(6)
            self.moves = {}

        def piece(self, which, half):
            lo, hi = self.cut[half], self.cut[half + 1]
            row = self.base + which * self.cut[2] + lo
            return part.at[pl.ds(pl.multiple_of(row, 8), hi - lo)]

        def first(self, side):
            half = side
            return self.r1.at[self.color, side, pl.ds(0, self.cut[half + 1] - self.cut[half])]

        def second(self, side, half):
            lo, hi = self.cut[half], self.cut[half + 1]
            return self.r2.at[self.color, side, pl.ds(lo, hi - lo)]

        def start(self):
            a, s = self.at, self.sem
            self.moves[0] = push(self.piece((a + 2) % 4, 0), self.first(0), self.plus, s)
            self.moves[1] = push(self.piece((a + 2) % 4, 1), self.first(1), self.minus, s + 1)
            self.moves[2] = push(self.piece((a + 1) % 4, 1), self.second(0, 1), self.plus, s + 2)
            self.moves[3] = push(self.piece((a + 3) % 4, 0), self.second(1, 0), self.minus, s + 3)

        def middle(self):
            a, s = self.at, self.sem
            self.moves[0].wait_recv()
            mine = self.piece((a + 1) % 4, 0)
            mine[...] = mine[...] + self.first(0)[...]
            self.moves[1].wait_recv()
            mine1 = self.piece((a + 3) % 4, 1)
            mine1[...] = mine1[...] + self.first(1)[...]
            self.moves[4] = push(mine, self.second(0, 0), self.plus, s + 4)
            self.moves[5] = push(mine1, self.second(1, 1), self.minus, s + 5)

        def finish(self):
            for n in (2, 3, 4, 5):
                self.moves[n].wait_recv()
            row = self.base + self.at * self.cut[2]
            mine = part.at[pl.ds(pl.multiple_of(row, 8), self.cut[2])]
            total = mine[...] + self.r2[self.color, 0] + self.r2[self.color, 1]
            return mine, total

    base_a, base_b = 0, HALF
    red = [
        Reduce(base_a, CUT_BIG, x, xp, xm, r1, r2, 0),
        Reduce(base_b, CUT_BIG, y, yp, ym, r1, r2, 1),
    ]
    for r in red:
        r.start()
    for r in red:
        r.middle()
    for r in red:
        mine, total = r.finish()
        mine[...] = total
    off_a = base_a + x * BIG + y * SMALL
    off_b = base_b + y * BIG + x * SMALL
    colors = (
        (base_a + x * BIG, y, (None, yp, yo, ym), off_a),
        (base_b + y * BIG, x, (None, xp, xo, xm), off_b),
    )
    cross = [sems(4), sems(4)]
    moves = []
    for n in (2, 1, 3):
        for color, (base, a, peer, _) in enumerate(colors):
            row = pl.multiple_of(base + ((a + n) % 4) * SMALL, 8)
            moves.append(push(part.at[pl.ds(row, SMALL)], r3.at[color, n], peer[n], cross[color] + n))
    for made in moves:
        made.wait_recv()
    for color, (base, a, peer, off) in enumerate(colors):
        mine = part.at[pl.ds(pl.multiple_of(off, 8), SMALL)]
        mine[...] = (mine[...] + r3[color, 2]) + (r3[color, 1] + r3[color, 3])

    load_q.wait()
    load_own.wait()

    def chunk(at):
        return qv.at[pl.ds(pl.multiple_of(at * 32, 32), 32)]

    sem_q = sems(4)
    source = (core == 1) & (x == y)
    receiver = (core == 1) & (x != y)

    @pl.when(jnp.logical_not(receiver))
    def _():
        qb[0] = qv[pl.ds(pl.multiple_of(x * 32, 32), 32), :]

    row_peers = (None, yp, yo, ym)
    for d in (1, 2, 3):

        @pl.when(source)
        def _():
            copy(chunk((y + d) % 4), qb.at[0], row_peers[d], sem_q + d, sem_q).start()

    def row_of(tile):
        late = tile // 9
        row = (1 - late) * (off_a + tile * 8) + late * (off_b + (tile - 9) * 8)
        return pl.multiple_of(row, 8)

    def tile_of(ref, tile):
        return ref.at[pl.ds(row_of(tile), 8)]

    my_held = held.at[core]
    sz, sz2 = sems(NZ), sems(NZ)
    for d in FAR_FIRST:
        dest = (z + d) % NZ
        push(tile_of(part, dest), zr.at[z], zs[d], sz + d, sz + z)
    for d in FAR_FIRST:
        dest = (z + d) % NZ

        @pl.when(dest < TILES - NZ)
        def _():
            copy(tile_of(part, dest + NZ), zr2.at[z], zs[d], sz2 + d, sz2 + z).start()

    zr[z] = part[pl.ds(row_of(z), 8), :]
    for d in FAR_FIRST:
        src = (z + NZ - d) % NZ
        copy(zr.at[src], zr.at[src], zs[d], sz + d, sz + src).wait_recv()
    total = zr[0]
    for n in range(1, NZ):
        total = total + zr[n]
    my_held[pl.ds(row_of(z), 8), :] = total

    @pl.when(z < TILES - NZ)
    def _():
        zr2[z] = part[pl.ds(row_of(z + NZ), 8), :]
        for d in FAR_FIRST:
            src = (z + NZ - d) % NZ
            copy(zr2.at[src], zr2.at[src], zs[d], sz2 + d, sz2 + src).wait_recv()
        total = zr2[0]
        for n in range(1, NZ):
            total = total + zr2[n]
        my_held[pl.ds(row_of(z + NZ), 8), :] = total

    gz, gz2 = sems(NZ), sems(NZ)
    mine = tile_of(my_held, z)
    for d in FAR_FIRST:
        push(mine, mine, zs[d], gz + d, gz + z)

    @pl.when(z < TILES - NZ)
    def _():
        mine = tile_of(my_held, z + NZ)
        for d in FAR_FIRST:
            copy(mine, mine, zs[d], gz2 + d, gz2 + z).start()

    for d in FAR_FIRST:
        src = (z + NZ - d) % NZ
        got = tile_of(my_held, src)
        copy(got, got, zs[d], gz + d, gz + src).wait_recv()
    for n in range(TILES - NZ):

        @pl.when(z != n)
        def _():
            got = tile_of(my_held, n + NZ)
            copy(got, got, zs[1], gz2 + 1, gz2 + n).wait_recv()

    class Gather:
        def __init__(self, get, whole, f, s, first, second):
            self.get, self.whole, self.f, self.s = get, whole, f, s
            self.first, self.second = first, second
            self.first_sem = sems(4)
            self.second_sem = [sems(6) for _ in range(4)]
            self.pair = sems(16)

        def chunk(self, n, m, half=None):
            at = (self.f + n) % 4, (self.s + m) % 4
            return self.whole(*at) if half is None else self.get(*at, half)

        def wait(self, ref, sem):
            copy(ref, ref, other, sem, sem).wait_recv()

        def start(self):
            mine = self.chunk(0, 0)
            for n in (1, 3, 2):
                push(mine, mine, self.first[n - 1], self.first_sem + n)

        def landed(self, n):
            self.wait(self.chunk(n, 0), self.first_sem + 4 - n)

        def send(self, n):
            sem = self.second_sem[n]
            plus, across, minus = self.second
            for device, half, k in ((plus, 0, 0), (minus, 1, 2), (plus, 1, 1), (minus, 0, 3)):
                ref = self.chunk(n, 0, half)
                push(ref, ref, device, sem + k)
            if n == 2:
                ref = self.chunk(n, 0)
                push(ref, ref, across, sem + 4)

        def forward(self, n):
            sem = self.second_sem[n]
            plus, _, minus = self.second
            for m, half, k, device in ((3, 0, 0, plus), (1, 1, 2, minus)):
                ref = self.chunk(n, m, half)
                self.wait(ref, sem + k)
                if n != 2:
                    push(ref, ref, device, sem + 4 + half)

        def near(self, n):
            sem = self.second_sem[n]
            self.wait(self.chunk(n, 3, 1), sem + 1)
            self.wait(self.chunk(n, 1, 0), sem + 3)
            self.hand(n, 3)
            self.hand(n, 1)

        def last(self, n):
            sem = self.second_sem[n]
            if n == 2:
                self.wait(self.chunk(n, 2), sem + 4)
            else:
                self.wait(self.chunk(n, 2, 0), sem + 4)
                self.wait(self.chunk(n, 2, 1), sem + 5)
            self.hand(n, 2)

        def paired(self, n, m):
            return self.chunk(n, m), self.pair + n * 4 + m

        def hand(self, n, m):
            ref, sem = self.paired(n, m)
            push(ref, ref, other, sem)

        def handed(self, n):
            for m in range(4):
                self.wait(*self.paired(n, m))

    def gather(both, ready):
        for g in both:
            g.start()
        for g in both:
            g.send(0)
            g.hand(0, 0)
        for n in (3, 1):
            for g in both:
                g.landed(n)
                g.send(n)
                g.hand(n, 0)
        for g in both:
            g.forward(0)
        for g in both:
            g.landed(2)
            g.send(2)
            g.hand(2, 0)
        for g in both:
            g.near(0)
        for g in both:
            g.forward(3)
        for g in both:
            g.last(0)
        for g in both:
            g.near(3)
        for g in both:
            g.forward(1)
        ready(0)
        for g in both:
            g.last(3)
        for g in both:
            g.near(1)
        ready(3)
        for g in both:
            g.last(1)
        ready(1)
        for g in both:
            g.forward(2)
            g.near(2)
        for g in both:
            g.last(2)
        ready(2)

    def held_rows(base):
        def get(f, s, half):
            lo, hi = CUT_SMALL[half], CUT_SMALL[half + 1]
            return my_held.at[pl.ds(pl.multiple_of(base + s * BIG + f * SMALL + lo, 8), hi - lo)]

        def whole(f, s):
            return my_held.at[pl.ds(pl.multiple_of(base + s * BIG + f * SMALL, 8), SMALL)]

        return get, whole

    sem_f = sems()

    @pl.when(receiver)
    def _():
        copy(qb.at[0], qb.at[0], yp, sem_q, sem_q).wait_recv()

    @pl.when(odd == 1)
    def _():
        copy(qb.at[0], qb.at[1], far, sem_f, sem_f).start()

    both = [
        Gather(*held_rows(base_a), y, x, (yp, yo, ym), (xp, xo, xm)),
        Gather(*held_rows(base_b), x, y, (xp, xo, xm), (yp, yo, ym)),
    ]
    gather(both, lambda n: None)
    for n in range(4):
        for g in both:
            g.handed(n)

    colsum[...] = jnp.zeros_like(colsum)
    trace = jnp.zeros((8, 128), F32)
    row_id = lax.broadcasted_iota(jnp.int32, (128, 128), 0)
    col_id = lax.broadcasted_iota(jnp.int32, (128, 128), 1)

    def place(block, i, j):
        at = (slice(i * 128, (i + 1) * 128), slice(j * 128, (j + 1) * 128))
        first = block.astype(BF16)
        left = block - first.astype(F32)
        second = left.astype(BF16)
        g0[at] = first
        g1[at] = second
        if i == j:
            third = jnp.where(row_id == col_id, left - second.astype(F32), 0.0)
            rest[:, at[1]] = jnp.sum(third, axis=0, keepdims=True)
        colsum[:, at[1]] += jnp.sum(jnp.abs(block).reshape(16, 8, 128), axis=0)

    for i in range(NB):
        for j in range(i, NB):
            owner, slot = SLOTS[i, j]
            block = held[owner, slot * 128 : (slot + 1) * 128, :]
            place(block, i, j)
            if i == j:
                diag = jnp.where(row_id == col_id, block, 0.0)
                trace = trace + jnp.sum(diag.reshape(16, 8, 128), axis=0)
            else:
                place(block.T, j, i)

    total_rows = ROWS * lax.axis_size("grp") * lax.axis_size("dev")
    scale = 1.0 / total_rows
    trace = jnp.sum(jnp.sum(trace, axis=0, keepdims=True), axis=1, keepdims=True)
    damp = DAMPING * trace / (total_rows * K)
    sums = jnp.sum(colsum[...], axis=0, keepdims=True) * scale
    bound = jnp.max(sums, axis=1, keepdims=True) + damp
    step = 1.0 / bound

    @pl.when(odd == 1)
    def _():
        copy(qb.at[0], qb.at[1], far, sem_f, sem_f).wait_recv()

    ys[...] = step * qb[odd].astype(F32)

    def iterate(_, carry):
        for n, value in enumerate(split3(ys[...])):
            xs[n * 32 : (n + 1) * 32, :] = value
        for n in range(4):
            at = slice(n * 256, (n + 1) * 256)
            mid = jnp.dot(xs[0:64], g1[:, at], preferred_element_type=F32)
            top = jnp.dot(xs[...], g0[:, at], preferred_element_type=F32)
            state = ys[:, at]
            prod = top[0:32] + (top[32:64] + mid[0:32] + (top[64:96] + mid[32:64] + state * rest[:, at]))
            query = qb[odd, :, at].astype(F32)
            ys[:, at] = state + step * (query - (prod * scale + damp * state))
        return carry

    lax.fori_loop(0, ITERS, iterate, 0)

    first_at, second_at = (1 - core) * y + core * x, (1 - core) * x + core * y

    def along(step, first):
        dx = step * (core if first else 1 - core)
        dy = step * (1 - core if first else core)
        return where((x + dx) % 4, (y + dy) % 4, z, core)

    pa[core, first_at, second_at] = ys[...].astype(BF16)

    out_sem = sems(8)
    send_near.wait_recv()
    kept = []

    def scores(far, n):
        which = (1 - far) * core + far * (1 - core)
        block = ((second_at if far else first_at) + n) % 4
        slot = far * 4 + n
        found = nt_dot(tq[...], pa[which, block].reshape(128, K)).astype(BF16)
        ob[slot, 0] = found[0:ROWS]
        ob[slot, 1] = found[ROWS : 2 * ROWS]
        col = pl.multiple_of((block * 4 + near_half * 2 + which) * 128, 128)
        push(ob.at[slot, 1], out_hbm.at[:, pl.ds(col, 128)], neighbour, out_sem + slot)
        keep = pltpu.make_async_copy(
            ob.at[slot, 0], out_hbm.at[:, pl.ds(col, 128)], local_sem.at[3 + slot]
        )
        keep.start()
        kept.append(keep)

    prepared = Gather(
        lambda f, s, h: pa.at[core, f, s, pl.ds(16 * h, 16)],
        lambda f, s: pa.at[core, f, s],
        first_at,
        second_at,
        [along(n, True) for n in (1, 2, 3)],
        [along(n, False) for n in (1, 2, 3)],
    )

    def handed(n):
        for m in range(4):
            ref = pa.at[1 - core, (second_at + n) % 4, (first_at + m) % 4]
            sem = prepared.pair + n * 4 + m
            copy(ref, ref, other, sem, sem).wait_recv()

    def ready(n):
        scores(0, n)
        if n in (3, 1):
            done = 0 if n == 3 else 3
            handed(done)
            scores(1, done)

    gather([prepared], ready)
    for n in (1, 2):
        handed(n)
        scores(1, n)
    for slot in range(8):
        far, n = slot // 4, slot % 4
        which = (1 - far) * core + far * (1 - core)
        block = ((second_at if far else first_at) + n) % 4
        col = pl.multiple_of((block * 4 + (1 - near_half) * 2 + which) * 128, 128)
        ref = out_hbm.at[:, pl.ds(col, 128)]
        copy(ob.at[slot, 1], ref, neighbour, out_sem + slot, out_sem + slot).wait_recv()

    for keep in kept:
        keep.wait()
    for made in started:
        made.wait_send()

    for d in (1, 2, 3):

        @pl.when(source)
        def _():
            copy(chunk((y + d) % 4), qb.at[0], row_peers[d], sem_q + d, sem_q).wait_send()

    @pl.when(odd == 1)
    def _():
        copy(qb.at[0], qb.at[1], far, sem_f, sem_f).wait_send()

    for d in FAR_FIRST:
        dest = (z + d) % NZ

        @pl.when(dest < TILES - NZ)
        def _():
            copy(tile_of(part, dest + NZ), zr2.at[z], zs[d], sz2 + d, sz2 + z).wait_send()

        @pl.when(z < TILES - NZ)
        def _():
            mine = tile_of(my_held, z + NZ)
            copy(mine, mine, zs[d], gz2 + d, gz2 + z).wait_send()


def body(train_grads, queries):
    nquery = queries.shape[0] * lax.axis_size("grp")
    return pl.pallas_call(
        kernel,
        out_shape=jax.ShapeDtypeStruct((ROWS, nquery), BF16),
        in_specs=[pl.BlockSpec(memory_space=pltpu.HBM)] * 2,
        out_specs=pl.BlockSpec(memory_space=pltpu.HBM),
        scratch_shapes=[
            pltpu.VMEM((2 * ROWS, K), BF16),
            pltpu.VMEM((2 * ROWS, K), BF16),
            pltpu.VMEM((ROWS, K), BF16),
            pltpu.VMEM((2, 32, K), BF16),
            pltpu.VMEM((HELD, 128), F32),
            pltpu.VMEM((2, HELD, 128), F32),
            pltpu.VMEM((2, 2, BIG // 2, 128), F32),
            pltpu.VMEM((2, 2, BIG, 128), F32),
            pltpu.VMEM((2, 4, SMALL, 128), F32),
            pltpu.VMEM((NZ, 8, 128), F32),
            pltpu.VMEM((NZ, 8, 128), F32),
            pltpu.VMEM((K, K), BF16),
            pltpu.VMEM((K, K), BF16),
            pltpu.VMEM((1, K), F32),
            pltpu.VMEM((8, K), F32),
            pltpu.VMEM((96, K), BF16),
            pltpu.VMEM((32, K), F32),
            pltpu.VMEM((2, 4, 4, 32, K), BF16),
            pltpu.VMEM((8, 2, ROWS, 128), BF16),
            pltpu.SemaphoreType.DMA((NSEM,)),
            pltpu.SemaphoreType.DMA((NSEM,)),
            pltpu.SemaphoreType.DMA((11,)),
        ],
        compiler_params=pltpu.CompilerParams(
            collective_id=0, has_side_effects=True, vmem_limit_bytes=63 * 1024 * 1024
        ),
    )(train_grads, queries)


def solution(mesh):
    return jax.shard_map(
        body,
        mesh=mesh,
        in_specs=(P(("grp", "dev"), None), P("grp", None)),
        out_specs=P(("grp", "dev"), None),
        check_vma=False,
    )
```

time: 106 us -> 93 us (0.88)
  Pallas kernels: 103 us -> 90.9 us
    pallas_call x1, Pallas kernels: 103 us -> 90.9 us  [body(): pl.pallas_call(kernel, out_shape=jax.ShapeDtypeStruct((ROWS, nquery), BF1...]
    unnamed x5 -> x1, local copies, waits for them, and re-layouts: 2.69 us -> 1.88 us
where the time goes in v2:
time: 93 us; the launch traced here: 92.8 us
  Pallas kernels  90.9 us (98%)
  local copies, waits for them, and re-layouts  1.88 us (2%)
    pallas_call x1, Pallas kernels, body(): pl.pallas_call(kernel, out_shape=jax.ShapeDtypeStruct((ROWS, nquery), BF1...  90.9 us
    unnamed x1, local copies, waits for them, and re-layouts  1.88 us

profile of v2, /device:TPU:1, one launch (start us, length us, event | category | flops | bytes accessed | tf_op | source)
XLA Modules:
  0.0 92.8 jit_solution(10398931968975751594)
XLA Ops:
  0.0 90.9 %shard_map.28 = bf16[128,2048]{1,0:T(8,128)(2,1)} custom-call(bf16[128,1024]{1,0:T(8,128)(2,1)} %t_hbm.1, bf16[128,1024]{1,0:T(8,128)(2,1)} %q_hbm.1), custom_call_target="tpu_custom_call" | custom-call | tf_op jit(solution)/shard_map/pallas_call | solution.py:572
  90.9 1.9 %copy.4 = bf16[128,2048]{1,0:T(8,128)(2,1)} copy(bf16[128,2048]{1,0:T(8,128)(2,1)} %shard_map.28) | data formatting | bytes 1048576

commit v3 on v2

--- a/solution.py
+++ b/solution.py
@@ -26,7 +26,6 @@
 SMALL = BIG // 4
 TILES = 2 * SMALL // 8
 CUT_BIG = (0, 144, 288)
-CUT_SMALL = (0, 40, 72)
 NSEM = 320
 FAR_FIRST = sorted(range(1, NZ), key=lambda d: -min(d, NZ - d))
 
@@ -45,7 +44,7 @@
 
 def kernel(
     t_hbm, q_hbm, out_hbm,
-    tt, tq, qv, qb, part, held, r1, r2, r3, zr, zr2, g0, g1, rest, colsum, xs, ys, pa, ob,
+    tt, tq, qv, qb, part, held, r1, r2, r3, zr, zr2, g0, g1, rest, colsum, trace, xs, ys, pa, ob,
     send_sem, recv_sem, local_sem,
 ):
     grp, dev = lax.axis_index("grp"), lax.axis_index("dev")
@@ -280,16 +279,15 @@
             copy(got, got, zs[1], gz2 + 1, gz2 + n).wait_recv()
 
     class Gather:
-        def __init__(self, get, whole, f, s, first, second):
-            self.get, self.whole, self.f, self.s = get, whole, f, s
+        def __init__(self, whole, f, s, first, second):
+            self.whole, self.f, self.s = whole, f, s
             self.first, self.second = first, second
             self.first_sem = sems(4)
-            self.second_sem = [sems(6) for _ in range(4)]
+            self.second_sem = [sems(4) for _ in range(4)]
             self.pair = sems(16)
 
-        def chunk(self, n, m, half=None):
-            at = (self.f + n) % 4, (self.s + m) % 4
-            return self.whole(*at) if half is None else self.get(*at, half)
+        def chunk(self, n, m):
+            return self.whole((self.f + n) % 4, (self.s + m) % 4)
 
         def wait(self, ref, sem):
             copy(ref, ref, other, sem, sem).wait_recv()
@@ -303,39 +301,14 @@
             self.wait(self.chunk(n, 0), self.first_sem + 4 - n)
 
         def send(self, n):
-            sem = self.second_sem[n]
-            plus, across, minus = self.second
-            for device, half, k in ((plus, 0, 0), (minus, 1, 2), (plus, 1, 1), (minus, 0, 3)):
-                ref = self.chunk(n, 0, half)
-                push(ref, ref, device, sem + k)
-            if n == 2:
-                ref = self.chunk(n, 0)
-                push(ref, ref, across, sem + 4)
-
-        def forward(self, n):
-            sem = self.second_sem[n]
-            plus, _, minus = self.second
-            for m, half, k, device in ((3, 0, 0, plus), (1, 1, 2, minus)):
-                ref = self.chunk(n, m, half)
-                self.wait(ref, sem + k)
-                if n != 2:
-                    push(ref, ref, device, sem + 4 + half)
-
-        def near(self, n):
-            sem = self.second_sem[n]
-            self.wait(self.chunk(n, 3, 1), sem + 1)
-            self.wait(self.chunk(n, 1, 0), sem + 3)
-            self.hand(n, 3)
-            self.hand(n, 1)
-
-        def last(self, n):
-            sem = self.second_sem[n]
-            if n == 2:
-                self.wait(self.chunk(n, 2), sem + 4)
-            else:
-                self.wait(self.chunk(n, 2, 0), sem + 4)
-                self.wait(self.chunk(n, 2, 1), sem + 5)
-            self.hand(n, 2)
+            ref = self.chunk(n, 0)
+            for m in (1, 3, 2):
+                push(ref, ref, self.second[m - 1], self.second_sem[n] + m)
+            self.hand(n, 0)
+
+        def arrived(self, n, m):
+            self.wait(self.chunk(n, m), self.second_sem[n] + 4 - m)
+            self.hand(n, m)
 
         def paired(self, n, m):
             return self.chunk(n, m), self.pair + n * 4 + m
@@ -353,53 +326,21 @@
             g.start()
         for g in both:
             g.send(0)
-            g.hand(0, 0)
-        for n in (3, 1):
+        for n in (3, 1, 2):
             for g in both:
                 g.landed(n)
                 g.send(n)
-                g.hand(n, 0)
-        for g in both:
-            g.forward(0)
-        for g in both:
-            g.landed(2)
-            g.send(2)
-            g.hand(2, 0)
-        for g in both:
-            g.near(0)
-        for g in both:
-            g.forward(3)
-        for g in both:
-            g.last(0)
-        for g in both:
-            g.near(3)
-        for g in both:
-            g.forward(1)
-        ready(0)
-        for g in both:
-            g.last(3)
-        for g in both:
-            g.near(1)
-        ready(3)
-        for g in both:
-            g.last(1)
-        ready(1)
-        for g in both:
-            g.forward(2)
-            g.near(2)
-        for g in both:
-            g.last(2)
-        ready(2)
+        for n in (0, 3, 1, 2):
+            for m in (3, 1, 2):
+                for g in both:
+                    g.arrived(n, m)
+            ready(n)
 
     def held_rows(base):
-        def get(f, s, half):
-            lo, hi = CUT_SMALL[half], CUT_SMALL[half + 1]
-            return my_held.at[pl.ds(pl.multiple_of(base + s * BIG + f * SMALL + lo, 8), hi - lo)]
-
         def whole(f, s):
             return my_held.at[pl.ds(pl.multiple_of(base + s * BIG + f * SMALL, 8), SMALL)]
 
-        return get, whole
+        return whole
 
     sem_f = sems()
 
@@ -412,16 +353,12 @@
         copy(qb.at[0], qb.at[1], far, sem_f, sem_f).start()
 
     both = [
-        Gather(*held_rows(base_a), y, x, (yp, yo, ym), (xp, xo, xm)),
-        Gather(*held_rows(base_b), x, y, (xp, xo, xm), (yp, yo, ym)),
+        Gather(held_rows(base_a), y, x, (yp, yo, ym), (xp, xo, xm)),
+        Gather(held_rows(base_b), x, y, (xp, xo, xm), (yp, yo, ym)),
     ]
     gather(both, lambda n: None)
-    for n in range(4):
-        for g in both:
-            g.handed(n)
-
     colsum[...] = jnp.zeros_like(colsum)
-    trace = jnp.zeros((8, 128), F32)
+    trace[...] = jnp.zeros_like(trace)
     row_id = lax.broadcasted_iota(jnp.int32, (128, 128), 0)
     col_id = lax.broadcasted_iota(jnp.int32, (128, 128), 1)
 
@@ -437,21 +374,37 @@
             rest[:, at[1]] = jnp.sum(third, axis=0, keepdims=True)
         colsum[:, at[1]] += jnp.sum(jnp.abs(block).reshape(16, 8, 128), axis=0)
 
-    for i in range(NB):
-        for j in range(i, NB):
-            owner, slot = SLOTS[i, j]
-            block = held[owner, slot * 128 : (slot + 1) * 128, :]
-            place(block, i, j)
-            if i == j:
-                diag = jnp.where(row_id == col_id, block, 0.0)
-                trace = trace + jnp.sum(diag.reshape(16, 8, 128), axis=0)
-            else:
-                place(block.T, j, i)
+    def place_owned(owner):
+        for i in OWNED[owner]:
+            for j in range(i, NB):
+                slot = SLOTS[i, j][1]
+                block = held[owner, slot * 128 : (slot + 1) * 128, :]
+                place(block, i, j)
+                if i == j:
+                    diag = jnp.where(row_id == col_id, block, 0.0)
+                    trace[...] += jnp.sum(diag.reshape(16, 8, 128), axis=0)
+                else:
+                    place(block.T, j, i)
+
+    for which in (0, 1):
+
+        @pl.when(core == which)
+        def _():
+            place_owned(which)
+
+    for n in range(4):
+        for g in both:
+            g.handed(n)
+    for which in (0, 1):
+
+        @pl.when(core != which)
+        def _():
+            place_owned(which)
 
     total_rows = ROWS * lax.axis_size("grp") * lax.axis_size("dev")
     scale = 1.0 / total_rows
-    trace = jnp.sum(jnp.sum(trace, axis=0, keepdims=True), axis=1, keepdims=True)
-    damp = DAMPING * trace / (total_rows * K)
+    trace_all = jnp.sum(jnp.sum(trace[...], axis=0, keepdims=True), axis=1, keepdims=True)
+    damp = DAMPING * trace_all / (total_rows * K)
     sums = jnp.sum(colsum[...], axis=0, keepdims=True) * scale
     bound = jnp.max(sums, axis=1, keepdims=True) + damp
     step = 1.0 / bound
@@ -506,7 +459,6 @@
         kept.append(keep)
 
     prepared = Gather(
-        lambda f, s, h: pa.at[core, f, s, pl.ds(16 * h, 16)],
         lambda f, s: pa.at[core, f, s],
         first_at,
         second_at,
@@ -590,6 +542,7 @@
             pltpu.VMEM((K, K), BF16),
             pltpu.VMEM((1, K), F32),
             pltpu.VMEM((8, K), F32),
+            pltpu.VMEM((8, 128), F32),
             pltpu.VMEM((96, K), BF16),
             pltpu.VMEM((32, K), F32),
             pltpu.VMEM((2, 4, 4, 32, K), BF16),

time: 93 us -> 89.1 us (0.958)
  Pallas kernels: 90.9 us -> 86.9 us
    pallas_call x1, Pallas kernels: 90.9 us -> 86.9 us  [body(): pl.pallas_call(kernel, out_shape=jax.ShapeDtypeStruct((ROWS, nquery), BF1...]
where the time goes in v3:
time: 89.1 us; the launch traced here: 88.8 us
  Pallas kernels  86.9 us (98%)
  local copies, waits for them, and re-layouts  1.88 us (2%)
    pallas_call x1, Pallas kernels, body(): pl.pallas_call(kernel, out_shape=jax.ShapeDtypeStruct((ROWS, nquery), BF1...  86.9 us
    unnamed x1, local copies, waits for them, and re-layouts  1.88 us

profile of v3, /device:TPU:1, one launch (start us, length us, event | category | flops | bytes accessed | tf_op | source)
XLA Modules:
  0.0 88.8 jit_solution(1850032784672598744)
XLA Ops:
  0.0 86.9 %shard_map.28 = bf16[128,2048]{1,0:T(8,128)(2,1)} custom-call(bf16[128,1024]{1,0:T(8,128)(2,1)} %t_hbm.1, bf16[128,1024]{1,0:T(8,128)(2,1)} %q_hbm.1), custom_call_target="tpu_custom_call" | custom-call | tf_op jit(solution)/shard_map/pallas_call | solution.py:524
  86.9 1.9 %copy.4 = bf16[128,2048]{1,0:T(8,128)(2,1)} copy(bf16[128,2048]{1,0:T(8,128)(2,1)} %shard_map.28) | data formatting | bytes 1048576

commit v4 on v3

--- a/solution.py
+++ b/solution.py
@@ -330,11 +330,15 @@
             for g in both:
                 g.landed(n)
                 g.send(n)
-        for n in (0, 3, 1, 2):
-            for m in (3, 1, 2):
+        for n, behind in ((0, None), (3, 0), (1, 3), (2, 1)):
+            for m in (3, 1):
                 for g in both:
                     g.arrived(n, m)
-            ready(n)
+            if behind is not None:
+                ready(behind)
+            for g in both:
+                g.arrived(n, 2)
+        ready(2)
 
     def held_rows(base):
         def whole(f, s):

time: 89.1 us -> 89.1 us (level)
  no operation moved by 1% of the time
where the time goes in v4:
time: 89.1 us; the launch traced here: 88.9 us
  Pallas kernels  87 us (98%)
  local copies, waits for them, and re-layouts  1.88 us (2%)
    pallas_call x1, Pallas kernels, body(): pl.pallas_call(kernel, out_shape=jax.ShapeDtypeStruct((ROWS, nquery), BF1...  87 us
    unnamed x1, local copies, waits for them, and re-layouts  1.88 us

profile of v4, /device:TPU:1, one launch (start us, length us, event | category | flops | bytes accessed | tf_op | source)
XLA Modules:
  0.0 88.9 jit_solution(11219823134368905810)
XLA Ops:
  0.0 87.0 %shard_map.28 = bf16[128,2048]{1,0:T(8,128)(2,1)} custom-call(bf16[128,1024]{1,0:T(8,128)(2,1)} %t_hbm.1, bf16[128,1024]{1,0:T(8,128)(2,1)} %q_hbm.1), custom_call_target="tpu_custom_call" | custom-call | tf_op jit(solution)/shard_map/pallas_call | solution.py:528
  87.0 1.9 %copy.4 = bf16[128,2048]{1,0:T(8,128)(2,1)} copy(bf16[128,2048]{1,0:T(8,128)(2,1)} %shard_map.28) | data formatting | bytes 1048576
